TPU v7x, 32 devices: a whole 2x2x4 slice. The times are simulated.
32 devices in a mesh: dp: 4 (over y, x), mp: 8 (over z, core).
Axes of the slice: x: 2, y: 2, z: 4, core: 2. Of those that a mesh axis runs over, the one named last changes fastest.
Arguments:
- grad_out: bfloat16 [4096, 2560], P(('dp', 'mp')), may hold values from -0.5 to 0.5
- hidden_act: bfloat16 [4096, 13824], P('dp', 'mp'), may hold values from -6 to 6
- carried: bfloat16 [4, 13824, 2560], P('dp', 'mp'), may hold values from -6 to 6
- prior_right: float32 [2560, 64], replicated, may hold values from -6 to 6
Outputs:
- residual_out: bfloat16 [4, 13824, 2560], P('dp', 'mp')
- next_right: float32 [2560, 64], replicated
All inputs are finite; a program needn't handle non-finite values.
Results may differ from a plain program's by a relative error of at most 0.0058.
Values may be sent and summed in bfloat16 or wider, within the bound.
A program may use at most 128 MiB of HBM per device.

v0:
```python
import jax
import jax.numpy as jnp
from jax import lax
from jax.sharding import PartitionSpec as P

highest = lax.Precision.HIGHEST
over_rows = (((0,), (0,)), ((), ()))


def ortho_from(gram_matrix, left_rows):
    rank_size = gram_matrix.shape[0]
    identity = jnp.eye(rank_size, dtype=jnp.float32)
    ridge_shift = 0.001 * jnp.trace(gram_matrix) / rank_size
    cholesky_factor = jnp.linalg.cholesky(gram_matrix + ridge_shift * identity)
    inverse = lax.linalg.triangular_solve(cholesky_factor, identity, left_side=True, lower=True)
    return jnp.dot(left_rows, inverse.T, precision=highest, preferred_element_type=jnp.float32)


def merged_block(grad_out, hidden_act, carried):
    weight_grad = lax.dot_general(
        hidden_act,
        lax.all_gather(grad_out, "mp", axis=0, tiled=True),
        over_rows,
        preferred_element_type=jnp.float32,
    )
    return carried[0].astype(jnp.float32) + weight_grad


def per_device(grad_out, hidden_act, carried, prior_right):
    out_proj = jnp.dot(
        grad_out.astype(jnp.float32),
        prior_right,
        precision=highest,
        preferred_element_type=jnp.float32,
    )
    gathered_proj = lax.all_gather(out_proj, "mp", axis=0, tiled=True)
    left_local = jnp.dot(
        carried[0].astype(jnp.float32),
        prior_right,
        precision=highest,
        preferred_element_type=jnp.float32,
    )
    left_local = left_local + lax.dot_general(
        hidden_act.astype(jnp.float32),
        gathered_proj,
        over_rows,
        precision=highest,
        preferred_element_type=jnp.float32,
    )
    left_whole = lax.psum(left_local.astype(jnp.bfloat16), "dp").astype(jnp.float32)
    gram_part = jnp.dot(
        left_whole.T, left_whole, precision=highest, preferred_element_type=jnp.float32
    )
    gram_matrix = lax.psum(gram_part, "mp")
    ortho_left = ortho_from(gram_matrix, left_whole)
    merged = merged_block(grad_out, hidden_act, carried)
    right_part = lax.dot_general(
        merged, ortho_left, over_rows, precision=highest, preferred_element_type=jnp.float32
    )
    next_right = lax.psum(right_part, ("dp", "mp")) / lax.axis_size("dp")
    low_rank = jnp.dot(
        ortho_left, next_right.T, precision=highest, preferred_element_type=jnp.float32
    )
    residual_out = (merged - low_rank).astype(jnp.bfloat16)[None]
    return (residual_out, next_right)


def solution(mesh):
    in_specs = (P(("dp", "mp"), None), P("dp", "mp"), P("dp", "mp", None), P())
    out_specs = (P("dp", "mp", None), P())
    return jax.shard_map(
        per_device, mesh=mesh, in_specs=in_specs, out_specs=out_specs, check_vma=False
    )
```

profile of v0, /device:TPU:25, one launch (start us, length us, event | category | flops | bytes accessed | tf_op | source)
XLA Modules:
  0.0 324.6 jit_solution(12680020227798394001)
XLA Ops:
  8.0 0.0 copy-start
  8.0 0.0 all-reduce.3.cloned.1.call-start
  8.1 2.1 fusion.9
  10.2 15.4 %all_gather.7 = f32[1024,64]{1,0:T(8,128)S(1)} all-gather(f32[128,64]{1,0:T(8,128)S(1)} %fusion.9), channel_id=1, replica_groups=mesh['dp'=4,'mp'=8] {'mp'}, dimensions={0}, use_global_device_ids=true | all-gather | bytes 294912 | tf_op jit(solution)/shard_map/all_gather | solution.py:36
  25.5 10.9 %fusion.1 = f32[1728,64]{0,1:T(8,128)S(1)} fusion(f32[2560,64]{0,1:T(8,128)} %param.7, bf16[1,1728,2560]{2,1,0:T(8,128)(2,1)} %param.6), kind=kOutput, calls=%fused_computation.3 | convolution fusion | flops 3397386240 | bytes 9945088 | tf_op jit(solution)/shard_map/dot_general | solution.py:37
  36.5 0.0 copy-done
  36.5 4.1 %fusion.4 = bf16[1728,64]{0,1:T(8,128)(2,1)} fusion(f32[1728,64]{0,1:T(8,128)S(1)} %fusion.1, f32[1024,64]{1,0:T(8,128)S(1)} %all_gather.7, bf16[1024,1728]{0,1:T(8,128)(2,1)S(1)} %copy-done), kind=kOutput, calls=%fused_computation.7 | convolution fusion | flops 1359175680 | bytes 4464640 | tf_op jit(solution)/shard_map/dot_general | solution.py:43
  40.5 0.0 all-reduce.3.cloned.1.call-update
  40.6 0.0 all-gather.2.cloned.1.call-start
  40.6 0.5 all-gather.2.cloned.1.call-update
  41.1 0.0 all-reduce.5.cloned.1.call-start
  41.2 42.6 %all-reduce.3.cloned.1.call-done = bf16[1728,64]{0,1:T(8,128)(2,1)} async-done(((bf16[1728,64]{0,1:T(8,128)(2,1)}), bf16[1728,64]{0,1:T(8,128)(2,1)}) %all-reduce.3.cloned.1.call-update) | async-done | bytes 221200 | tf_op jit(solution)/shard_map/psum | solution.py:50
  83.8 1.9 fusion.10
  85.7 27.1 %psum.22 = f32[64,64]{1,0:T(8,128)} all-reduce(f32[64,64]{1,0:T(8,128)} %fusion.10), channel_id=1, replica_groups=mesh['dp'=4,'mp'=8] {'mp'}, use_global_device_ids=true, to_apply=%region_1.0 | all-reduce | flops 4096 | bytes 32768 | tf_op jit(solution)/shard_map/psum | solution.py:54
  112.7 1.4 select_reduce_fusion.1
  114.8 1.4 select_add_fusion
  116.1 1.4 copy.6
  117.6 1.4 fusion.8
  119.0 7.2 %cholesky.18 = f32[64,64]{1,0:T(8,128)} custom-call(f32[64,64]{1,0:T(8,128)} %fusion.8), custom_call_target="Cholesky" | custom-call | tf_op jit(solution)/shard_map/jit(cholesky)/cholesky | solution.py:14
  126.2 0.8 select_reduce_fusion
  127.0 0.6 compare_reduce_fusion
  127.6 2.0 fusion.5
  129.7 6.3 %custom-call.6 = f32[1,64,64]{1,2,0:T(8,128)} custom-call(f32[1,64,64]{2,1,0:T(8,128)} %fusion.5), custom_call_target="InvertDiagBlocksLowerTriangular" | custom-call | tf_op jit(solution)/shard_map/triangular_solve | solution.py:15
  136.0 1.0 fusion.6
  136.9 2.1 fusion.11
  139.0 0.0 all-gather.2.cloned.1.call-done
  139.0 0.0 copy-start.1
  139.0 16.3 %convert_add_fusion = f32[1728,2560]{1,0:T(8,128)} fusion(bf16[1024,1728]{0,1:T(8,128)(2,1)S(1)} %copy-done, bf16[1024,2560]{1,0:T(8,128)(2,1)} %all-gather.2.cloned.1.call-done, bf16[1,1728,2560]{2,1,0:T(8,128)(2,1)} %param.6), kind=kOutput, calls=%fused_computation.1 | convolution fusion | flops 9068544000 | bytes 35323904 | tf_op jit(solution)/shard_map/dot_general | solution.py:20
  155.3 0.0 copy-done.1
  155.3 14.4 %fusion.12 = f32[2560,64]{0,1:T(8,128)} fusion(f32[1728,2560]{1,0:T(8,128)} %convert_add_fusion, f32[1728,64]{0,1:T(8,128)S(1)} %copy-done.1), kind=kOutput, calls=%fused_computation.24 | convolution fusion | flops 3397386240 | bytes 18792448 | tf_op jit(solution)/shard_map/dot_general | solution.py:57
  169.7 0.0 all-reduce.5.cloned.1.call-update
  169.8 127.6 %all-reduce.5.cloned.1.call-done = f32[2560,64]{0,1:T(8,128)} async-done(((f32[2560,64]{0,1:T(8,128)}), f32[2560,64]{0,1:T(8,128)}) %all-reduce.5.cloned.1.call-update) | async-done | bytes 655376 | tf_op jit(solution)/shard_map/psum | solution.py:60
  297.4 1.1 broadcast_multiply_fusion
  298.5 0.0 copy-start.2
  298.5 18.6 %fusion = bf16[1,1728,2560]{2,1,0:T(8,128)(2,1)} fusion(f32[1728,2560]{1,0:T(8,128)} %convert_add_fusion, f32[1728,64]{0,1:T(8,128)} %fusion.11, f32[2560,64]{0,1:T(8,128)S(1)} %broadcast_multiply_fusion), kind=kOutput, calls=%fused_computation.2 | convolution fusion | flops 3406233600 | bytes 27639808 | tf_op jit(solution)/shard_map/dot_general | solution.py:61
  317.2 0.0 copy-done.2
Async XLA Ops:
  8.0 28.5 %copy-start = (bf16[1024,1728]{0,1:T(8,128)(2,1)S(1)}, bf16[1024,1728]{0,1:T(8,128)(2,1)}, u32[]{:S(2)}) copy-start(bf16[1024,1728]{0,1:T(8,128)(2,1)} %param.5) | copy-start | bytes 10616836
  8.0 75.8 %all-reduce.3.cloned.1.call-start = ((), (), s32[]{:S(2)}) async-start(), calls=%async_computation.1 | async-start | bytes 458752 | tf_op jit(solution)/shard_map/psum | solution.py:50
  40.6 98.4 %all-gather.2.cloned.1.call-start = ((), (), s32[]{:S(2)}) async-start(), calls=%async_computation | async-start | bytes 5898240 | tf_op jit(solution)/shard_map/all_gather | solution.py:22
  41.1 256.2 %all-reduce.5.cloned.1.call-start = ((), (), s32[]{:S(2)}) async-start(), calls=%async_computation.2 | async-start | bytes 1310720 | tf_op jit(solution)/shard_map/psum | solution.py:60
  139.0 16.4 %copy-start.1 = (f32[1728,64]{0,1:T(8,128)S(1)}, f32[1728,64]{0,1:T(8,128)}, u32[]{:S(2)}) copy-start(f32[1728,64]{0,1:T(8,128)} %fusion.11) | copy-start | bytes 1327108
  298.5 18.6 %copy-start.2 = (f32[2560,64]{0,1:T(8,128)}, f32[2560,64]{0,1:T(8,128)S(1)}, u32[]{:S(2)}) copy-start(f32[2560,64]{0,1:T(8,128)S(1)} %broadcast_multiply_fusion) | copy-start | bytes 1966084
Sparse Core Ops, SparseCore 0:
  40.7 43.0 all-reduce.2
  169.9 127.4 all-reduce.4
Sparse Core Ops, SparseCore 1:
  42.7 54.4 all-gather.1
where the time goes:
time: 330 us; the launch traced here: 325 us
  waiting for transfers between devices  171 us (52%)
  matrix products  71.3 us (22%)
  blocking collectives  42.5 us (13%)
  other arithmetic  22.2 us (7%)
  between operations  16.2 us (5%)
    psum x1, waiting for transfers between devices, per_device(): next_right = lax.psum(right_part, ('dp', 'mp')) / lax.axis_size('dp')  128 us
    psum x1, waiting for transfers between devices, per_device(): lax.psum(left_local.astype(jnp.bfloat16), 'dp').astype(jnp.float32)  42.6 us
    psum x1, blocking collectives, per_device(): gram_matrix = lax.psum(gram_part, 'mp')  27.1 us
    dot_general x1, matrix products, per_device(): jnp.dot(ortho_left, next_right.T, precision=highest, preferred_element_ty...  18.6 us
    dot_general x1, matrix products, merged_block(): lax.dot_general(hidden_act, lax.all_gather(grad_out, 'mp', axis=0, tiled=...  16.3 us
    all_gather x1, blocking collectives, per_device(): gathered_proj = lax.all_gather(out_proj, 'mp', axis=0, tiled=True)  15.4 us
    dot_general x1, matrix products, per_device(): lax.dot_general(merged, ortho_left, over_rows, precision=highest, preferr...  14.4 us
    dot_general x1, matrix products, per_device(): jnp.dot(carried[0].astype(jnp.float32), prior_right, precision=highest, p...  10.9 us
  transfers between devices with their start and end apart: 3, of which 2 were waited for; matrix products, arithmetic and copies ran while one was open for 8% of the time, Pallas kernels for 0%

commit v1 on v0

v1 whole, which is shorter than its diff:
```python
import functools

import jax
import jax.numpy as jnp
from jax import lax
from jax.experimental import pallas as pl
from jax.experimental.pallas import tpu as pltpu
from jax.sharding import PartitionSpec as P

highest = lax.Precision.HIGHEST
over_rows = (((0,), (0,)), ((), ()))
F32, BF16 = jnp.float32, jnp.bfloat16


def lane_tiles(extent, step):
    return [(s, min(step, extent - s)) for s in range(0, extent, step)]


def split2(x, axis):
    hi = x.astype(BF16)
    lo = (x - hi.astype(F32)).astype(BF16)
    return jnp.concatenate([hi, lo], axis=axis)


def halves(x, rank):
    return x[:, :rank] + x[:, rank:]


def inverse_factor(gram):
    n = gram.shape[0]
    ri = lax.broadcasted_iota(jnp.int32, (n, 2 * n), 0)
    ci = lax.broadcasted_iota(jnp.int32, (n, 2 * n), 1)
    eye = (ri == ci)[:, :n]
    trace = jnp.sum(jnp.sum(jnp.where(eye, gram, 0.0), axis=1, keepdims=True), axis=0, keepdims=True)
    ridged = gram + jnp.where(eye, 0.001 * (trace / n), 0.0)
    start = jnp.concatenate([ridged, jnp.where(eye, 1.0, 0.0)], axis=1)

    def step(k, a):
        row = jnp.sum(jnp.where(ri == k, a, 0.0), axis=0, keepdims=True)
        col = jnp.sum(jnp.where(ci == k, a, 0.0), axis=1, keepdims=True)
        piv = jnp.sum(jnp.where(ci[:1] == k, row, 0.0), axis=1, keepdims=True)
        r = 1.0 / jnp.sqrt(piv)
        scaled = row * r
        return jnp.where(ri == k, scaled, jnp.where(ri > k, a - (col * r) * scaled, a))

    return lax.fori_loop(0, n, step, start)[:, n:]


def fused_kernel(dp, mp, g_hbm, h_hbm, c_hbm, p_ref, merged_hbm, l2_ref, a2_ref, nr_ref,
                 h_v, c_v, m_v, gall, p2, pj, x_v, lbuf, l_v, gbuf, racc, rsend, rrecv,
                 dbuf, abuf, local_sem, out_sem, pj_s, pj_r, g_s, g_r, l_s, l_r,
                 gr_s, gr_r, rs_s, rs_r, d_s, d_r, a_s, a_r):
    tok, dim = g_hbm.shape
    rank = p_ref.shape[1]
    ff = c_hbm.shape[0]
    half = ff // 2
    me_d, me_m = lax.axis_index("dp"), lax.axis_index("mp")

    def push(src_of, dst, size, axis, me, send, recv):
        copies = []
        for k in range(1, size):
            peer = lax.rem(me + k, size)
            copies.append(pltpu.make_async_remote_copy(
                src_ref=src_of(peer), dst_ref=dst.at[me], send_sem=send.at[k],
                recv_sem=recv.at[me], device_id={axis: peer},
                device_id_type=pl.DeviceIdType.MESH))
            copies[-1].start()
        return copies

    def arrive(dst, size, axis, me, send, recv):
        for k in range(1, size):
            peer = lax.rem(me + k, size)
            pltpu.make_async_remote_copy(
                src_ref=dst.at[peer], dst_ref=dst.at[peer], send_sem=send.at[k],
                recv_sem=recv.at[peer], device_id={axis: peer},
                device_id_type=pl.DeviceIdType.MESH).wait_recv()

    own = pltpu.make_async_copy(g_hbm, gall.at[me_m], local_sem.at[0])
    own.start()
    load_c = pltpu.make_async_copy(c_hbm, c_v, local_sem.at[1])
    load_c.start()
    load_h = pltpu.make_async_copy(h_hbm, h_v, local_sem.at[2])
    load_h.start()

    barrier = pltpu.get_barrier_semaphore()
    for k in range(1, mp):
        pl.semaphore_signal(barrier, inc=1, device_id={"mp": lax.rem(me_m + k, mp)},
                            device_id_type=pl.DeviceIdType.MESH)
    for k in range(1, dp):
        pl.semaphore_signal(barrier, inc=1, device_id={"dp": lax.rem(me_d + k, dp)},
                            device_id_type=pl.DeviceIdType.MESH)

    p2[...] = split2(p_ref[...], 1)
    own.wait()
    proj = halves(jnp.dot(gall[me_m], p2[...], preferred_element_type=F32), rank)
    pj[me_m] = split2(proj, 1)
    pl.semaphore_wait(barrier, mp + dp - 2)

    sent = push(lambda peer: pj.at[me_m], pj, mp, "mp", me_m, pj_s, pj_r)
    sent += push(lambda peer: g_hbm, gall, mp, "mp", me_m, g_s, g_r)

    load_c.wait()
    for s in (0, half):
        x_v[s:s + half, :] = jnp.dot(c_v[s:s + half, :], p2[...], preferred_element_type=F32)
    load_h.wait()
    arrive(pj, mp, "mp", me_m, pj_s, pj_r)
    pj_all = pj[...].reshape(mp * tok, 2 * rank)
    for s, w in lane_tiles(ff, 256):
        x_v[s:s + w, :] += lax.dot_general(h_v[:, s:s + w], pj_all, over_rows,
                                           preferred_element_type=F32)
    lbuf[me_d] = jnp.concatenate(
        [halves(x_v[:half, :], rank), halves(x_v[half:, :], rank)], axis=1).astype(BF16)
    sent += push(lambda peer: lbuf.at[me_d], lbuf, dp, "dp", me_d, l_s, l_r)
    arrive(lbuf, dp, "dp", me_d, l_s, l_r)
    packed = lbuf[0].astype(F32)
    for k in range(1, dp):
        packed = packed + lbuf[k].astype(F32)
    packed = packed.astype(BF16)
    l_v[:half, :] = packed[:, :rank]
    l_v[half:, :] = packed[:, rank:]
    l2_ref[...] = jnp.concatenate([l_v[...], l_v[...]], axis=1)
    gram = lax.dot_general(l_v[...], l_v[...], over_rows, preferred_element_type=F32)
    gbuf[me_m] = jnp.concatenate([gram, gram], axis=1)
    sent += push(lambda peer: gbuf.at[me_m], gbuf, mp, "mp", me_m, gr_s, gr_r)

    arrive(gall, mp, "mp", me_m, g_s, g_r)
    racc[...] = jnp.zeros_like(racc)
    outs = []
    for t, (s, w) in enumerate(lane_tiles(ff, 256)):
        @pl.loop(0, dim // 512)
        def _(n, s=s, w=w):
            cols = pl.ds(pl.multiple_of(n * 512, 512), 512)
            tile = c_v[s:s + w, cols].astype(F32) + lax.dot_general(
                h_v[:, s:s + w], gall[:, :, cols].reshape(mp * tok, 512), over_rows,
                preferred_element_type=F32)
            m_v[s:s + w, cols] = tile
            racc[:, cols] += lax.dot_general(l_v[s:s + w, :], tile.astype(BF16), over_rows,
                                             preferred_element_type=F32)
        outs.append(pltpu.make_async_copy(
            m_v.at[pl.ds(s, w)], merged_hbm.at[pl.ds(s, w)], out_sem.at[t]))
        outs[-1].start()

    part = rank // mp
    for j in range(mp):
        rsend[j] = racc[j * part:(j + 1) * part, :]
    sent += push(lambda peer: rsend.at[peer], rrecv, mp, "mp", me_m, rs_s, rs_r)

    arrive(gbuf, mp, "mp", me_m, gr_s, gr_r)
    gram = gbuf[0]
    for j in range(1, mp):
        gram = gram + gbuf[j]
    inverse = inverse_factor(gram[:, :rank])

    arrive(rrecv, mp, "mp", me_m, rs_s, rs_r)
    acc = rsend[me_m]
    for k in range(1, mp):
        acc = acc + rrecv[lax.rem(me_m + k, mp)]
    dbuf[me_d] = acc
    sent += push(lambda peer: dbuf.at[me_d], dbuf, dp, "dp", me_d, d_s, d_r)
    arrive(dbuf, dp, "dp", me_d, d_s, d_r)
    acc = dbuf[0]
    for k in range(1, dp):
        acc = acc + dbuf[k]
    abuf[me_m] = acc
    sent += push(lambda peer: abuf.at[me_m], abuf, mp, "mp", me_m, a_s, a_r)
    arrive(abuf, mp, "mp", me_m, a_s, a_r)
    for j in range(mp):
        racc[j * part:(j + 1) * part, :] = abuf[j]
    right = jnp.dot(inverse, racc[...], precision=highest, preferred_element_type=F32) / dp
    nr_ref[...] = right
    coef = lax.dot_general(inverse, right, over_rows, precision=highest,
                           preferred_element_type=F32)
    a2_ref[...] = split2(coef, 0)
    for c in sent:
        c.wait_send()
    for c in outs:
        c.wait()


def per_device(dp, mp, grad_out, hidden_act, carried, prior_right):
    tok, dim = grad_out.shape
    rank = prior_right.shape[1]
    ff = hidden_act.shape[1]
    toks = hidden_act.shape[0]
    part = rank // mp
    dma = pltpu.SemaphoreType.DMA
    anywhere = pl.BlockSpec(memory_space=pl.ANY)
    vmem = pl.BlockSpec(memory_space=pltpu.VMEM)
    merged, left2, coef2, right_t = pl.pallas_call(
        functools.partial(fused_kernel, dp, mp),
        out_shape=(
            jax.ShapeDtypeStruct((ff, dim), F32),
            jax.ShapeDtypeStruct((ff, 2 * rank), BF16),
            jax.ShapeDtypeStruct((2 * rank, dim), BF16),
            jax.ShapeDtypeStruct((rank, dim), F32),
        ),
        in_specs=[anywhere, anywhere, anywhere, vmem],
        out_specs=(anywhere, vmem, vmem, vmem),
        scratch_shapes=[
            pltpu.VMEM((toks, ff), BF16),
            pltpu.VMEM((ff, dim), BF16),
            pltpu.VMEM((ff, dim), F32),
            pltpu.VMEM((mp, tok, dim), BF16),
            pltpu.VMEM((dim, 2 * rank), BF16),
            pltpu.VMEM((mp, tok, 2 * rank), BF16),
            pltpu.VMEM((ff, 2 * rank), F32),
            pltpu.VMEM((dp, ff // 2, 2 * rank), BF16),
            pltpu.VMEM((ff, rank), BF16),
            pltpu.VMEM((mp, rank, 2 * rank), F32),
            pltpu.VMEM((rank, dim), F32),
            pltpu.VMEM((mp, part, dim), F32),
            pltpu.VMEM((mp, part, dim), F32),
            pltpu.VMEM((dp, part, dim), F32),
            pltpu.VMEM((mp, part, dim), F32),
            dma((3,)),
            dma((len(lane_tiles(ff, 256)),)),
            dma((mp,)), dma((mp,)), dma((mp,)), dma((mp,)),
            dma((dp,)), dma((dp,)),
            dma((mp,)), dma((mp,)), dma((mp,)), dma((mp,)),
            dma((dp,)), dma((dp,)), dma((mp,)), dma((mp,)),
        ],
        compiler_params=pltpu.CompilerParams(
            collective_id=0, has_side_effects=True, vmem_limit_bytes=62 * 1024 * 1024),
    )(grad_out, hidden_act, carried[0], prior_right)
    low_rank = jnp.dot(left2, coef2, preferred_element_type=F32)
    residual_out = (merged - low_rank).astype(BF16)[None]
    return (residual_out, right_t.T)


def solution(mesh):
    in_specs = (P(("dp", "mp"), None), P("dp", "mp"), P("dp", "mp", None), P())
    out_specs = (P("dp", "mp", None), P())
    return jax.shard_map(
        functools.partial(per_device, mesh.shape["dp"], mesh.shape["mp"]),
        mesh=mesh, in_specs=in_specs, out_specs=out_specs, check_vma=False
    )
```

time: 330 us -> 208 us (0.63); the launches traced: 325 us -> 208 us
  Pallas kernels: 0 us -> 186 us
  waiting for transfers between devices: 171 us -> 0 us
  matrix products: 71.3 us -> 12.4 us
  blocking collectives: 42.5 us -> 0 us
  other arithmetic: 22.2 us -> 0 us
  between operations: 16.2 us -> 0.65 us
  local copies, waits for them, and re-layouts: 1.46 us -> 9.21 us
    pallas_call x0 -> x1, Pallas kernels: none -> 186 us  [per_device(): pl.pallas_call(functools.partial(fused_kernel, dp, mp), out_shape=(jax.Sh...]
    psum x2 -> x0, waiting for transfers between devices: 170 us -> none  [the longest x1 128 us: per_device(): next_right = lax.psum(right_part, ('dp', 'mp')) / lax.axis_size('dp')]
    dot_general x8 -> x1, matrix products: 70.4 us -> 12.4 us  [per_device(): low_rank = jnp.dot(left2, coef2, preferred_element_type=F32)]
    psum x1 -> x0, blocking collectives: 27.1 us -> none  [per_device(): gram_matrix = lax.psum(gram_part, 'mp')]
    another operation x5 -> x0, other arithmetic: 17 us -> none  [the longest x3 8.65 us: ortho_from(): cholesky_factor = jnp.linalg.cholesky(gram_matrix + ridge_shift * identity)]
    all_gather x1 -> x0, blocking collectives: 15.4 us -> none  [per_device(): gathered_proj = lax.all_gather(out_proj, 'mp', axis=0, tiled=True)]
    unnamed x6 -> x5, local copies, waits for them, and re-layouts: 0.02 us -> 9.21 us
  transfers between devices with their start and end apart: 3 -> 0, of which waited for: 2 -> 0; matrix products, arithmetic and copies ran while one was open for 8% -> 0% of each run, Pallas kernels for 0% -> 0%
where the time goes in v1:
time: 208 us
  Pallas kernels  186 us (89%)
  matrix products  12.4 us (6%)
  local copies, waits for them, and re-layouts  9.21 us (4%)
    pallas_call x1, Pallas kernels, per_device(): pl.pallas_call(functools.partial(fused_kernel, dp, mp), out_shape=(jax.Sh...  186 us
    dot_general x1, matrix products, per_device(): low_rank = jnp.dot(left2, coef2, preferred_element_type=F32)  12.4 us
    unnamed x5, local copies, waits for them, and re-layouts  9.21 us

profile of v1, /device:TPU:25, one launch (start us, length us, event | category | flops | bytes accessed | tf_op | source)
XLA Modules:
  0.0 208.0 jit_solution(8476273883258983310)
XLA Ops:
  0.6 2.6 %copy.7.p_ref = f32[2560,64]{1,0:T(8,128)} copy(f32[2560,64]{0,1:T(8,128)} %param.7) | data formatting | bytes 1310720 | tf_op args[3]
  3.2 5.8 %copy.6.h_hbm = bf16[1024,1728]{1,0:T(8,128)(2,1)} copy(bf16[1024,1728]{0,1:T(8,128)(2,1)} %param.5) | data formatting | bytes 7077888 | tf_op args[1]
  9.0 185.7 %shard_map.59 = (f32[1728,2560]{1,0:T(8,128)}, bf16[1728,128]{1,0:T(8,128)(2,1)}, bf16[128,2560]{1,0:T(8,128)(2,1)}, f32[64,2560]{1,0:T(8,128)}) custom-call(bf16[128,2560]{1,0:T(8,128)(2,1)} %g_hbm.1, bf16[1024,1728]{1,0:T(8,128)(2,1)} %copy.6.h_hbm, bf16[1728,2560]{1,0:T(8,128)(2,1)} %bitcast.6, f32[2560,64]{1,0:T(8,128)} %copy.7.p_ref), custom_call_target="tpu_custom_call" | custom-call | tf_op jit(solution)/shard_map/pallas_call | solution.py:189
  194.8 0.0 copy-start
  194.8 12.4 %fusion = bf16[1,1728,2560]{2,1,0:T(8,128)(2,1)} fusion(f32[1728,2560]{1,0:T(8,128)} %get-tuple-element.6, bf16[1728,128]{1,0:T(8,128)(2,1)} %get-tuple-element.7, bf16[128,2560]{1,0:T(8,128)(2,1)} %get-tuple-element.8), kind=kOutput, calls=%fused_computation.1 | convolution fusion | flops 1141309440 | bytes 27639808 | tf_op jit(solution)/shard_map/dot_general | solution.py:225
  207.2 0.0 copy-done
  207.2 0.8 copy.9
Async XLA Ops:
  194.8 12.5 %copy-start = (f32[64,2560]{1,0:T(8,128)S(1)}, f32[64,2560]{1,0:T(8,128)}, u32[]{:S(2)}) copy-start(f32[64,2560]{1,0:T(8,128)} %get-tuple-element.9) | copy-start | bytes 1966084

commit v2 on v1

--- a/solution.py
+++ b/solution.py
@@ -47,11 +47,11 @@
 
 
 def fused_kernel(dp, mp, g_hbm, h_hbm, c_hbm, p_ref, merged_hbm, l2_ref, a2_ref, nr_ref,
-                 h_v, c_v, m_v, gall, p2, pj, x_v, lbuf, l_v, gbuf, racc, rsend, rrecv,
+                 h_v, c_v, m_v, gall, p2, pj, x_v, lbuf, l_v, gbuf, racc, rsend, rpair, rsum, rrecv,
                  dbuf, abuf, local_sem, out_sem, pj_s, pj_r, g_s, g_r, l_s, l_r,
-                 gr_s, gr_r, rs_s, rs_r, d_s, d_r, a_s, a_r):
+                 gr_s, gr_r, rs_s, rs_r, pair_r, d_s, d_r, a_s, a_r):
     tok, dim = g_hbm.shape
-    rank = p_ref.shape[1]
+    rank = p_ref.shape[0]
     ff = c_hbm.shape[0]
     half = ff // 2
     me_d, me_m = lax.axis_index("dp"), lax.axis_index("mp")
@@ -75,6 +75,42 @@
                 recv_sem=recv.at[peer], device_id={axis: peer},
                 device_id_type=pl.DeviceIdType.MESH).wait_recv()
 
+    core = lax.rem(me_m, 2)
+    me_z = me_m // 2
+    partner = me_m + 1 - 2 * core
+    chips = mp // 2
+
+    def to_mp(src, dst, send, recv, peer):
+        return pltpu.make_async_remote_copy(
+            src_ref=src, dst_ref=dst, send_sem=send, recv_sem=recv,
+            device_id={"mp": peer}, device_id_type=pl.DeviceIdType.MESH)
+
+    def gather_start(src, buf, send, recv):
+        copies = []
+        for k in range(1, chips):
+            copies.append(to_mp(src, buf.at[me_m], send.at[k], recv.at[me_m],
+                                lax.rem(me_m + 2 * k, mp)))
+        copies.append(to_mp(src, buf.at[me_m], send.at[0], recv.at[me_m], partner))
+        for c in copies:
+            c.start()
+        return copies
+
+    def gather_finish(buf, send, recv):
+        copies = []
+        for step in range(1, chips):
+            k = (step + 1) // 2 if step % 2 else chips - step // 2
+            block = lax.rem(me_m + 2 * k, mp)
+            to_mp(buf.at[block], buf.at[block], send.at[chips + k], recv.at[block],
+                  partner).wait_recv()
+            copies.append(to_mp(buf.at[block], buf.at[block], send.at[chips + k],
+                                recv.at[block], partner))
+            copies[-1].start()
+        for k in range(chips):
+            block = lax.rem(partner + 2 * k, mp)
+            to_mp(buf.at[block], buf.at[block], send.at[0], recv.at[block],
+                  partner).wait_recv()
+        return copies
+
     own = pltpu.make_async_copy(g_hbm, gall.at[me_m], local_sem.at[0])
     own.start()
     load_c = pltpu.make_async_copy(c_hbm, c_v, local_sem.at[1])
@@ -90,24 +126,23 @@
         pl.semaphore_signal(barrier, inc=1, device_id={"dp": lax.rem(me_d + k, dp)},
                             device_id_type=pl.DeviceIdType.MESH)
 
-    p2[...] = split2(p_ref[...], 1)
+    p2[...] = split2(p_ref[...].T, 1)
     own.wait()
     proj = halves(jnp.dot(gall[me_m], p2[...], preferred_element_type=F32), rank)
     pj[me_m] = split2(proj, 1)
     pl.semaphore_wait(barrier, mp + dp - 2)
 
-    sent = push(lambda peer: pj.at[me_m], pj, mp, "mp", me_m, pj_s, pj_r)
-    sent += push(lambda peer: g_hbm, gall, mp, "mp", me_m, g_s, g_r)
+    sent = gather_start(pj.at[me_m], pj, pj_s, pj_r)
+    sent += gather_start(g_hbm, gall, g_s, g_r)
 
     load_c.wait()
     for s in (0, half):
         x_v[s:s + half, :] = jnp.dot(c_v[s:s + half, :], p2[...], preferred_element_type=F32)
     load_h.wait()
-    arrive(pj, mp, "mp", me_m, pj_s, pj_r)
+    sent += gather_finish(pj, pj_s, pj_r)
     pj_all = pj[...].reshape(mp * tok, 2 * rank)
     for s, w in lane_tiles(ff, 256):
-        x_v[s:s + w, :] += lax.dot_general(h_v[:, s:s + w], pj_all, over_rows,
-                                           preferred_element_type=F32)
+        x_v[s:s + w, :] += jnp.dot(h_v[s:s + w, :], pj_all, preferred_element_type=F32)
     lbuf[me_d] = jnp.concatenate(
         [halves(x_v[:half, :], rank), halves(x_v[half:, :], rank)], axis=1).astype(BF16)
     sent += push(lambda peer: lbuf.at[me_d], lbuf, dp, "dp", me_d, l_s, l_r)
@@ -121,17 +156,17 @@
     l2_ref[...] = jnp.concatenate([l_v[...], l_v[...]], axis=1)
     gram = lax.dot_general(l_v[...], l_v[...], over_rows, preferred_element_type=F32)
     gbuf[me_m] = jnp.concatenate([gram, gram], axis=1)
-    sent += push(lambda peer: gbuf.at[me_m], gbuf, mp, "mp", me_m, gr_s, gr_r)
-
-    arrive(gall, mp, "mp", me_m, g_s, g_r)
+    sent += gather_start(gbuf.at[me_m], gbuf, gr_s, gr_r)
+
+    sent += gather_finish(gall, g_s, g_r)
     racc[...] = jnp.zeros_like(racc)
     outs = []
     for t, (s, w) in enumerate(lane_tiles(ff, 256)):
         @pl.loop(0, dim // 512)
         def _(n, s=s, w=w):
             cols = pl.ds(pl.multiple_of(n * 512, 512), 512)
-            tile = c_v[s:s + w, cols].astype(F32) + lax.dot_general(
-                h_v[:, s:s + w], gall[:, :, cols].reshape(mp * tok, 512), over_rows,
+            tile = c_v[s:s + w, cols].astype(F32) + jnp.dot(
+                h_v[s:s + w, :], gall[:, :, cols].reshape(mp * tok, 512),
                 preferred_element_type=F32)
             m_v[s:s + w, cols] = tile
             racc[:, cols] += lax.dot_general(l_v[s:s + w, :], tile.astype(BF16), over_rows,
@@ -142,19 +177,28 @@
 
     part = rank // mp
     for j in range(mp):
-        rsend[j] = racc[j * part:(j + 1) * part, :]
-    sent += push(lambda peer: rsend.at[peer], rrecv, mp, "mp", me_m, rs_s, rs_r)
-
-    arrive(gbuf, mp, "mp", me_m, gr_s, gr_r)
+        rsend[j % 2, j // 2] = racc[j * part:(j + 1) * part, :]
+    pair = to_mp(rsend.at[1 - core], rpair, rs_s.at[0], pair_r, partner)
+    pair.start()
+    sent += gather_finish(gbuf, gr_s, gr_r)
+    pair.wait()
+    for z in range(chips):
+        rsum[z] = rsend[core, z] + rpair[z]
+    for k in range(1, chips):
+        z = lax.rem(me_z + k, chips)
+        c = to_mp(rsum.at[z], rrecv.at[me_z], rs_s.at[k], rs_r.at[me_z], 2 * z + core)
+        c.start()
+        sent.append(c)
     gram = gbuf[0]
     for j in range(1, mp):
         gram = gram + gbuf[j]
     inverse = inverse_factor(gram[:, :rank])
 
-    arrive(rrecv, mp, "mp", me_m, rs_s, rs_r)
-    acc = rsend[me_m]
-    for k in range(1, mp):
-        acc = acc + rrecv[lax.rem(me_m + k, mp)]
+    acc = rsum[me_z]
+    for k in range(1, chips):
+        z = lax.rem(me_z + k, chips)
+        to_mp(rrecv.at[z], rrecv.at[z], rs_s.at[k], rs_r.at[z], 2 * z + core).wait_recv()
+        acc = acc + rrecv[z]
     dbuf[me_d] = acc
     sent += push(lambda peer: dbuf.at[me_d], dbuf, dp, "dp", me_d, d_s, d_r)
     arrive(dbuf, dp, "dp", me_d, d_s, d_r)
@@ -162,8 +206,8 @@
     for k in range(1, dp):
         acc = acc + dbuf[k]
     abuf[me_m] = acc
-    sent += push(lambda peer: abuf.at[me_m], abuf, mp, "mp", me_m, a_s, a_r)
-    arrive(abuf, mp, "mp", me_m, a_s, a_r)
+    sent += gather_start(abuf.at[me_m], abuf, a_s, a_r)
+    sent += gather_finish(abuf, a_s, a_r)
     for j in range(mp):
         racc[j * part:(j + 1) * part, :] = abuf[j]
     right = jnp.dot(inverse, racc[...], precision=highest, preferred_element_type=F32) / dp
@@ -197,7 +241,7 @@
         in_specs=[anywhere, anywhere, anywhere, vmem],
         out_specs=(anywhere, vmem, vmem, vmem),
         scratch_shapes=[
-            pltpu.VMEM((toks, ff), BF16),
+            pltpu.VMEM((ff, toks), BF16),
             pltpu.VMEM((ff, dim), BF16),
             pltpu.VMEM((ff, dim), F32),
             pltpu.VMEM((mp, tok, dim), BF16),
@@ -208,20 +252,22 @@
             pltpu.VMEM((ff, rank), BF16),
             pltpu.VMEM((mp, rank, 2 * rank), F32),
             pltpu.VMEM((rank, dim), F32),
-            pltpu.VMEM((mp, part, dim), F32),
-            pltpu.VMEM((mp, part, dim), F32),
+            pltpu.VMEM((2, mp // 2, part, dim), F32),
+            pltpu.VMEM((mp // 2, part, dim), F32),
+            pltpu.VMEM((mp // 2, part, dim), F32),
+            pltpu.VMEM((mp // 2, part, dim), F32),
             pltpu.VMEM((dp, part, dim), F32),
             pltpu.VMEM((mp, part, dim), F32),
             dma((3,)),
             dma((len(lane_tiles(ff, 256)),)),
             dma((mp,)), dma((mp,)), dma((mp,)), dma((mp,)),
             dma((dp,)), dma((dp,)),
-            dma((mp,)), dma((mp,)), dma((mp,)), dma((mp,)),
+            dma((mp,)), dma((mp,)), dma((mp // 2,)), dma((mp // 2,)), dma,
             dma((dp,)), dma((dp,)), dma((mp,)), dma((mp,)),
         ],
         compiler_params=pltpu.CompilerParams(
             collective_id=0, has_side_effects=True, vmem_limit_bytes=62 * 1024 * 1024),
-    )(grad_out, hidden_act, carried[0], prior_right)
+    )(grad_out, hidden_act.T, carried[0], prior_right.T)
     low_rank = jnp.dot(left2, coef2, preferred_element_type=F32)
     residual_out = (merged - low_rank).astype(BF16)[None]
     return (residual_out, right_t.T)

time: 208 us -> 131 us (0.63)
  Pallas kernels: 186 us -> 117 us
  local copies, waits for them, and re-layouts: 9.21 us -> 0.84 us
    pallas_call x1, Pallas kernels: 186 us -> 117 us  [per_device(): pl.pallas_call(functools.partial(fused_kernel, dp, mp), out_shape=(jax.Sh...]
    unnamed x5 -> x3, local copies, waits for them, and re-layouts: 9.21 us -> 0.84 us
where the time goes in v2:
time: 131 us
  Pallas kernels  117 us (89%)
  matrix products  12.4 us (9%)
    pallas_call x1, Pallas kernels, per_device(): pl.pallas_call(functools.partial(fused_kernel, dp, mp), out_shape=(jax.Sh...  117 us
    dot_general x1, matrix products, per_device(): low_rank = jnp.dot(left2, coef2, preferred_element_type=F32)  12.4 us

profile of v2, /device:TPU:25, one launch (start us, length us, event | category | flops | bytes accessed | tf_op | source)
XLA Modules:
  0.0 130.6 jit_solution(1984252570156542798)
XLA Ops:
  0.6 116.7 %shard_map.59 = (f32[1728,2560]{1,0:T(8,128)}, bf16[1728,128]{1,0:T(8,128)(2,1)}, bf16[128,2560]{1,0:T(8,128)(2,1)}, f32[64,2560]{1,0:T(8,128)}) custom-call(bf16[128,2560]{1,0:T(8,128)(2,1)} %g_hbm.1, bf16[1728,1024]{1,0:T(8,128)(2,1)} %bitcast.9, bf16[1728,2560]{1,0:T(8,128)(2,1)} %bitcast.8, f32[64,2560]{1,0:T(8,128)} %bitcast.11), custom_call_target="tpu_custom_call" | custom-call | tf_op jit(solution)/shard_map/pallas_call | solution.py:233
  117.3 0.0 copy-start
  117.3 12.4 %fusion = bf16[1,1728,2560]{2,1,0:T(8,128)(2,1)} fusion(f32[1728,2560]{1,0:T(8,128)} %get-tuple-element.6, bf16[1728,128]{1,0:T(8,128)(2,1)} %get-tuple-element.7, bf16[128,2560]{1,0:T(8,128)(2,1)} %get-tuple-element.8), kind=kOutput, calls=%fused_computation.1 | convolution fusion | flops 1141309440 | bytes 27639808 | tf_op jit(solution)/shard_map/dot_general | solution.py:271
  129.8 0.0 copy-done
  129.8 0.8 copy.7
Async XLA Ops:
  117.3 12.4 %copy-start = (f32[64,2560]{1,0:T(8,128)S(1)}, f32[64,2560]{1,0:T(8,128)}, u32[]{:S(2)}) copy-start(f32[64,2560]{1,0:T(8,128)} %get-tuple-element.9) | copy-start | bytes 1966084
